TPU v7x, 32 devices: a whole 2x2x4 slice. The times are simulated.
32 devices in a mesh: dp: 16 (over z, y, x), seq: 2 (over core).
Axes of the slice: x: 2, y: 2, z: 4, core: 2. Of those that a mesh axis runs over, the one named last changes fastest.
Arguments:
- chains_in: bfloat16 [128, 160, 768], P(('dp', 'seq')), may hold values from -6 to 6
- lengths: int32 [128], P(('dp', 'seq')), may hold values from 95 to 160
- d_out: bfloat16 [128, 160, 768], P(('dp', 'seq')), may hold values from -6 to 6
- w_query: bfloat16 [768, 768], replicated, may hold values from -0.21875 to 0.21875
- b_query: float32 [768], replicated, may hold values from -3 to 3
- w_key: bfloat16 [768, 768], replicated, may hold values from -0.21875 to 0.21875
- w_value: bfloat16 [768, 768], replicated, may hold values from -0.21875 to 0.21875
- b_value: float32 [768], replicated, may hold values from -3 to 3
- w_output: bfloat16 [768, 768], replicated, may hold values from -2.5 to 2.5
- b_output: float32 [768], replicated, may hold values from -3 to 3
- gain_one: float32 [768], replicated, may hold values from 0.25 to 1.75
- shift_one: float32 [768], replicated, may hold values from -2 to 2
- w_inner: bfloat16 [768, 3072], replicated, may hold values from -0.21875 to 0.21875
- b_inner: float32 [3072], replicated, may hold values from -3 to 3
- w_outer: bfloat16 [3072, 768], replicated, may hold values from -0.109375 to 0.109375
- b_outer: float32 [768], replicated, may hold values from -3 to 3
- gain_two: float32 [768], replicated, may hold values from 0.25 to 1.75
- shift_two: float32 [768], replicated, may hold values from -2 to 2
Outputs:
- layer_out: bfloat16 [128, 160, 768], P(('dp', 'seq'))
- d_x: float32 [128, 160, 768], P(('dp', 'seq'))
- d_w_query: float32 [768, 768], replicated
- d_b_query: float32 [768], replicated
- d_w_key: float32 [768, 768], replicated
- d_w_value: float32 [768, 768], replicated
- d_b_value: float32 [768], replicated
- d_w_output: float32 [768, 768], replicated
- d_b_output: float32 [768], replicated
- d_gain_one: float32 [768], replicated
- d_shift_one: float32 [768], replicated
- d_w_inner: float32 [768, 3072], replicated
- d_b_inner: float32 [3072], replicated
- d_w_outer: float32 [3072, 768], replicated
- d_b_outer: float32 [768], replicated
- d_gain_two: float32 [768], replicated
- d_shift_two: float32 [768], replicated
Inputs may be any that keep to these rules, and one draw needn't show every extreme that they name: `lengths`: every chain fills more than half of its 160 positions.
All inputs are finite; a program needn't handle non-finite values.
Results may differ from a plain program's by a relative error of at most 0.015.
Values may be sent and summed in bfloat16 or wider, within the bound.
No kernel may reach another device: no remote copies, remote signals or barrier semaphores. Data moves between devices by JAX's collectives and lax.ppermute only.
A program may use at most 256 MiB of HBM per device.

v0:
```python
import jax
import jax.numpy as jnp
from jax import lax
from jax.sharding import PartitionSpec as P

H = 12
EPS = 1e-12


def norm_forward(h, gain, shift):
    centre = h - jnp.mean(h, -1, keepdims=True)
    scale = lax.rsqrt(jnp.mean(centre * centre, -1, keepdims=True) + EPS)
    unit = centre * scale
    return (unit * gain + shift, unit, scale)


def norm_backward(grad, unit, scale, gain):
    d_gain = jnp.sum(grad * unit, 0)
    d_shift = jnp.sum(grad, 0)
    inner = grad * gain
    d_h = scale * (
        inner
        - jnp.mean(inner, -1, keepdims=True)
        - unit * jnp.mean(inner * unit, -1, keepdims=True)
    )
    return (d_h, d_gain, d_shift)


def over_rows(left, right):
    return lax.dot_general(
        left, right, (((0,), (0,)), ((), ())), preferred_element_type=jnp.float32
    )


def times_trans(left, weight):
    return lax.dot_general(
        left, weight, (((1,), (1,)), ((), ())), preferred_element_type=jnp.float32
    )


def attn_scores(query, keys, live_keys):
    seqs, count, width = query.shape
    total = keys.shape[1]
    size = width // H
    q_heads = query.reshape(seqs, count, H, size)
    k_heads = keys.reshape(seqs, total, H, size)
    scores = (
        jnp.einsum("bqhe,bkhe->bhqk", q_heads, k_heads, preferred_element_type=jnp.float32) * 0.125
    )
    return jnp.where(live_keys[:, None, None, :], scores, -1000000000.0)


def packed(grads, count):
    flat = jnp.concatenate([g.reshape(-1) for g in grads])
    extra = -flat.shape[0] % count
    return flat.reshape(count, -1)


def unpacked(flat, grads):
    flat = flat.reshape(-1)
    pieces = []
    start = 0
    for grad in grads:
        number = grad.size
        pieces.append(flat[start : start + number].reshape(grad.shape))
        start = start + number
    return tuple(pieces)


def body(
    chains_in,
    lengths,
    d_out,
    w_query,
    b_query,
    w_key,
    w_value,
    b_value,
    w_output,
    b_output,
    gain_one,
    shift_one,
    w_inner,
    b_inner,
    w_outer,
    b_outer,
    gain_two,
    shift_two,
):
    f32 = jnp.float32
    low_type = jnp.bfloat16
    seqs, length, width = chains_in.shape
    rows = seqs * length
    size = width // H
    parts = lax.axis_size("dp")
    count = lax.axis_size("dp") * lax.axis_size("seq")
    place = jnp.arange(length, dtype=jnp.int32)
    live_rows = place[None, :] < lengths[:, None]
    flat_x = chains_in.reshape(rows, width)
    query = (
        (jnp.dot(flat_x, w_query, preferred_element_type=f32) + b_query)
        .astype(low_type)
        .reshape(seqs, length, width)
    )
    keys = (
        jnp.dot(flat_x, w_key, preferred_element_type=f32)
        .astype(low_type)
        .reshape(seqs, length, width)
    )
    values = (
        (jnp.dot(flat_x, w_value, preferred_element_type=f32) + b_value)
        .astype(low_type)
        .reshape(seqs, length, width)
    )
    scores = attn_scores(query, keys, live_rows)
    top = jnp.max(scores, -1, keepdims=True)
    expo = jnp.exp(scores - top)
    summed = jnp.sum(expo, -1, keepdims=True)
    prob_b = (expo / summed).astype(low_type)
    lse = top + jnp.log(summed)
    v_heads = values.reshape(seqs, length, H, size)
    mixed = (
        jnp.einsum("bhqk,bkhe->bqhe", prob_b, v_heads, preferred_element_type=f32)
        .reshape(rows, width)
        .astype(low_type)
    )
    h_one = flat_x.astype(f32) + jnp.dot(mixed, w_output, preferred_element_type=f32) + b_output
    first, unit_one, scale_one = norm_forward(h_one, gain_one, shift_one)
    live_flat = live_rows.reshape(rows)
    fin = first.astype(low_type)
    pre = jnp.dot(fin, w_inner, preferred_element_type=f32) + b_inner
    hidden = jax.nn.gelu(pre, approximate=False).astype(low_type)
    ffn_home = (jnp.dot(hidden, w_outer, preferred_element_type=f32) + b_outer).astype(low_type)
    h_two = first + ffn_home.astype(f32)
    second, unit_two, scale_two = norm_forward(h_two, gain_two, shift_two)
    keep = live_flat[:, None].astype(f32)
    layer_out = (second * keep).astype(low_type).reshape(seqs, length, width)
    grad_out = d_out.reshape(rows, width).astype(f32) * keep
    d_h_two, d_gain_two, d_shift_two = norm_backward(grad_out, unit_two, scale_two, gain_two)
    d_ffn = d_h_two.astype(low_type)
    d_w_outer = over_rows(hidden, d_ffn)
    d_b_outer = jnp.sum(d_ffn.astype(f32), 0)
    d_hidden = times_trans(d_ffn, w_outer)
    gelu_pull = jax.vjp(lambda z: jax.nn.gelu(z, approximate=False), pre)[1]
    d_pre = gelu_pull(d_hidden)[0].astype(low_type)
    d_w_inner = over_rows(fin, d_pre)
    d_b_inner = jnp.sum(d_pre.astype(f32), 0)
    d_fin = times_trans(d_pre, w_inner).astype(low_type)
    d_home = d_fin
    d_first = d_h_two + d_home.astype(f32)
    ffn_grads = (d_w_inner, d_b_inner, d_w_outer, d_b_outer, d_gain_two, d_shift_two)
    d_h_one, d_gain_one, d_shift_one = norm_backward(d_first, unit_one, scale_one, gain_one)
    d_attn = d_h_one.astype(low_type)
    d_w_output = over_rows(mixed, d_attn)
    d_b_output = jnp.sum(d_attn.astype(f32), 0)
    d_mixed = times_trans(d_attn, w_output).astype(low_type).reshape(seqs, length, H, size)
    scores = attn_scores(query, keys, live_rows)
    prob = jnp.exp(scores - lse)
    prob_b = prob.astype(low_type)
    d_prob = jnp.einsum("bqhe,bkhe->bhqk", d_mixed, v_heads, preferred_element_type=f32)
    delta = jnp.sum(prob * d_prob, -1, keepdims=True)
    d_scores = (prob * (d_prob - delta)).astype(low_type)
    k_heads = keys.reshape(seqs, length, H, size)
    q_heads = query.reshape(seqs, length, H, size)
    d_query = (
        (jnp.einsum("bhqk,bkhe->bqhe", d_scores, k_heads, preferred_element_type=f32) * 0.125)
        .astype(low_type)
        .reshape(rows, width)
    )
    d_key = (
        (jnp.einsum("bhqk,bqhe->bkhe", d_scores, q_heads, preferred_element_type=f32) * 0.125)
        .astype(low_type)
        .reshape(rows, width)
    )
    d_value = (
        jnp.einsum("bhqk,bqhe->bkhe", prob_b, d_mixed, preferred_element_type=f32)
        .astype(low_type)
        .reshape(rows, width)
    )
    d_w_query = over_rows(flat_x, d_query)
    d_b_query = jnp.sum(d_query.astype(f32), 0)
    d_w_key = over_rows(flat_x, d_key)
    d_w_value = over_rows(flat_x, d_value)
    d_b_value = jnp.sum(d_value.astype(f32), 0)
    d_x = (
        d_h_one
        + times_trans(d_query, w_query)
        + times_trans(d_key, w_key)
        + times_trans(d_value, w_value)
    )
    d_x = d_x.reshape(seqs, length, width)
    attn_grads = (
        d_w_query,
        d_b_query,
        d_w_key,
        d_w_value,
        d_b_value,
        d_w_output,
        d_b_output,
        d_gain_one,
        d_shift_one,
    )
    local_grads = attn_grads + ffn_grads
    big = [g for g in local_grads if g.ndim == 2]
    small = [g for g in local_grads if g.ndim == 1]
    sums = lax.psum(jnp.concatenate(small), ("dp", "seq"))
    small_sums = unpacked(sums, small)
    big_sums = []
    for grad in big:
        part = lax.psum_scatter(
            grad.astype(low_type), ("dp", "seq"), scatter_dimension=0, tiled=True
        )
        big_sums.append(lax.all_gather(part, ("dp", "seq"), axis=0, tiled=True).astype(f32))
    every = []
    for grad in local_grads:
        every.append(big_sums.pop(0) if grad.ndim == 2 else small_sums[0])
        small_sums = small_sums if grad.ndim == 2 else small_sums[1:]
    return (
        layer_out,
        d_x,
        every[0],
        every[1],
        every[2],
        every[3],
        every[4],
        every[5],
        every[6],
        every[7],
        every[8],
        every[9],
        every[10],
        every[11],
        every[12],
        every[13],
        every[14],
    )


def solution(mesh):
    return jax.shard_map(
        body,
        mesh=mesh,
        in_specs=(
            P(("dp", "seq"), None, None),
            P(("dp", "seq")),
            P(("dp", "seq"), None, None),
            P(),
            P(),
            P(),
            P(),
            P(),
            P(),
            P(),
            P(),
            P(),
            P(),
            P(),
            P(),
            P(),
            P(),
            P(),
        ),
        out_specs=(
            P(("dp", "seq"), None, None),
            P(("dp", "seq"), None, None),
            P(),
            P(),
            P(),
            P(),
            P(),
            P(),
            P(),
            P(),
            P(),
            P(),
            P(),
            P(),
            P(),
            P(),
            P(),
        ),
        check_vma=False,
    )
```

profile of v0, /device:TPU:0, one launch (start us, length us, event | category | flops | bytes accessed | tf_op | source)
XLA Modules:
  0.0 1139.7 jit_solution(12008616428699110538)
XLA Ops:
  7.2 2.6 add_convert_fusion.3
  9.8 2.6 reshape.191
  12.5 4.6 copy.78
  17.1 2.5 add_convert_fusion.2
  19.6 2.6 reshape.192
  22.2 4.5 copy.76
  26.8 2.5 convolution_convert_fusion.8
  29.3 2.6 reshape.193
  31.9 3.5 copy.77
  35.4 3.6 fusion.12
  39.0 2.0 fusion.6
  42.2 2.5 fusion.20
  44.7 2.4 copy.80
  47.0 4.1 convert_element_type.174
  51.2 2.6 fusion.46
  53.8 1.3 copy-done.8
  55.6 23.9 %multiply_convert_fusion.1 = (bf16[640,3072]{1,0:T(8,128)(2,1)S(1)}, f32[640,3072]{1,0:T(8,128)}, f32[640,3072]{1,0:T(8,128)}) fusion(f32[3072]{0:T(1024)S(1)} %copy-done.22, bf16[768,3072]{1,0:T(8,128)(2,1)} %param.30, f32[640,768]{1,0:T(8,128)} %copy-done.8, f32[768]{0:T(1024)S(1)} %copy-done.26, f32[768]{0:T(1024)S(1)} %copy-done.19, ...), kind=kOutput, calls=%fused_computation.7 | convolution fusion | flops 3152117760 | bytes 26369024 | tf_op jit(solution)/shard_map/dot_general | solution.py:131
  79.5 7.2 fusion.47
  87.2 1.5 copy-done.5
  90.2 3.3 convert_reduce_fusion.3
  93.5 11.6 %convert_reduce_fusion = (f32[3072]{0:T(1024)S(1)}, bf16[640,3072]{1,0:T(8,128)(2,1)S(1)}) fusion(f32[640,3072]{1,0:T(8,128)} %get-tuple-element.64, bf16[3072,768]{1,0:T(8,128)(2,1)} %param.32, f32[640,768]{1,0:T(8,128)S(1)} %get-tuple-element.60, f32[640,3072]{1,0:T(8,128)} %get-tuple-element.80, f32[3072]{0:T(1024)S(1)} %copy-done.22), kind=kOutput, calls=%fused_computation.2 | convolution fusion | flops 3053810688 | bytes 26370048 | tf_op jit(solution)/shard_map/dot_general | solution.py:36
  105.2 3.8 multiply_reduce_fusion.2
  109.7 1.3 copy-done.6
  110.9 2.0 convolution_convert_fusion.7
  112.9 4.1 reshape.194
  117.0 4.6 copy.82
  121.6 7.5 multiply_reduce_fusion
  129.1 4.9 multiply_convert_fusion
  137.1 1.8 reshape.179
  138.9 3.6 fusion.26
  142.5 2.5 copy.100
  145.1 3.5 fusion.25
  148.6 1.2 copy.89
  149.8 1.8 reshape.180
  151.6 3.6 fusion.27
  155.2 2.5 copy.102
  157.8 5.5 convert_reduce_fusion.1
  164.5 2.0 reshape.181
  166.5 3.6 fusion.28
  170.1 2.5 copy.104
  172.8 3.3 convolution_convert_fusion.2
  176.2 9.1 convolution_convert_fusion.1
  185.3 8.8 convolution_convert_fusion
  194.3 49.8 %reduce-scatter.19.cloned.1.call-done = bf16[24,768]{1,0:T(8,128)(2,1)} async-done(((bf16[768,768]{1,0:T(8,128)(2,1)}), bf16[24,768]{1,0:T(8,128)(2,1)}) %reduce-scatter.19.cloned.1.call-update) | async-done | bytes 36880 | tf_op jit(solution)/shard_map/reduce_scatter | solution.py:210
  244.2 100.9 %reduce-scatter.21.cloned.1.call-done = bf16[24,768]{1,0:T(8,128)(2,1)} async-done(((bf16[768,768]{1,0:T(8,128)(2,1)}), bf16[24,768]{1,0:T(8,128)(2,1)}) %reduce-scatter.21.cloned.1.call-update) | async-done | bytes 36880 | tf_op jit(solution)/shard_map/reduce_scatter | solution.py:210
  345.1 100.4 %reduce-scatter.23.cloned.1.call-done = bf16[24,768]{1,0:T(8,128)(2,1)} async-done(((bf16[768,768]{1,0:T(8,128)(2,1)}), bf16[24,768]{1,0:T(8,128)(2,1)}) %reduce-scatter.23.cloned.1.call-update) | async-done | bytes 36880 | tf_op jit(solution)/shard_map/reduce_scatter | solution.py:210
  445.6 100.8 %reduce-scatter.13.cloned.1.call-done = bf16[24,768]{1,0:T(8,128)(2,1)} async-done(((bf16[768,768]{1,0:T(8,128)(2,1)}), bf16[24,768]{1,0:T(8,128)(2,1)}) %reduce-scatter.13.cloned.1.call-update) | async-done | bytes 36880 | tf_op jit(solution)/shard_map/reduce_scatter | solution.py:210
  546.4 111.9 %reduce-scatter.15.cloned.1.call-done = bf16[24,3072]{1,0:T(8,128)(2,1)} async-done(((bf16[768,3072]{1,0:T(8,128)(2,1)}), bf16[24,3072]{1,0:T(8,128)(2,1)}) %reduce-scatter.15.cloned.1.call-update) | async-done | bytes 147472 | tf_op jit(solution)/shard_map/reduce_scatter | solution.py:210
  658.4 112.9 %reduce-scatter.17.cloned.1.call-done = bf16[96,768]{1,0:T(8,128)(2,1)} async-done(((bf16[3072,768]{1,0:T(8,128)(2,1)}), bf16[96,768]{1,0:T(8,128)(2,1)}) %reduce-scatter.17.cloned.1.call-update) | async-done | bytes 147472 | tf_op jit(solution)/shard_map/reduce_scatter | solution.py:210
  771.5 40.6 %psum.7 = f32[9216]{0:T(1024)S(1)} all-reduce(f32[9216]{0:T(1024)S(1)} %constant_dynamic-update-slice_fusion), channel_id=1, replica_groups=mesh['dp'=16,'seq'=2] {'dp','seq'}, use_global_device_ids=true, to_apply=%region_21.22 | all-reduce | flops 9216 | bytes 73728 | tf_op jit(solution)/shard_map/psum | solution.py:206
  813.4 2.7 fusion.49
  817.7 2.3 add_add_fusion
  820.0 7.2 all-gather.7.cloned.1.call-done
  827.3 2.8 convert_element_type.202
  830.1 53.1 %all-gather.9.cloned.1.call-done = bf16[768,768]{1,0:T(8,128)(2,1)} async-done(((bf16[24,768]{1,0:T(8,128)(2,1)}), bf16[768,768]{1,0:T(8,128)(2,1)}) %all-gather.9.cloned.1.call-update) | async-done | bytes 1179664 | tf_op jit(solution)/shard_map/all_gather | solution.py:213
  883.2 2.8 convert_element_type.210
  886.0 53.1 %all-gather.11.cloned.1.call-done = bf16[768,768]{1,0:T(8,128)(2,1)} async-done(((bf16[24,768]{1,0:T(8,128)(2,1)}), bf16[768,768]{1,0:T(8,128)(2,1)}) %all-gather.11.cloned.1.call-update) | async-done | bytes 1179664 | tf_op jit(solution)/shard_map/all_gather | solution.py:213
  939.1 2.8 convert_element_type.213
  941.9 52.9 %all-gather.13.cloned.1.call-done = bf16[768,768]{1,0:T(8,128)(2,1)} async-done(((bf16[24,768]{1,0:T(8,128)(2,1)}), bf16[768,768]{1,0:T(8,128)(2,1)}) %all-gather.13.cloned.1.call-update) | async-done | bytes 1179664 | tf_op jit(solution)/shard_map/all_gather | solution.py:213
  994.8 2.8 convert_element_type.215
  997.7 62.7 %all-gather.15.cloned.1.call-done = bf16[768,3072]{1,0:T(8,128)(2,1)} async-done(((bf16[24,3072]{1,0:T(8,128)(2,1)}), bf16[768,3072]{1,0:T(8,128)(2,1)}) %all-gather.15.cloned.1.call-update) | async-done | bytes 4718608 | tf_op jit(solution)/shard_map/all_gather | solution.py:213
  1060.4 7.4 convert_element_type.217
  1067.7 57.9 %all-gather.17.cloned.1.call-done = bf16[3072,768]{1,0:T(8,128)(2,1)} async-done(((bf16[96,768]{1,0:T(8,128)(2,1)}), bf16[3072,768]{1,0:T(8,128)(2,1)}) %all-gather.17.cloned.1.call-update) | async-done | bytes 4718608 | tf_op jit(solution)/shard_map/all_gather | solution.py:213
  1125.6 6.8 convert_element_type.219
  (118 shorter events, 12.3 us)
Async XLA Ops:
  7.2 43.9 %copy-start = (bf16[768,768]{1,0:T(8,128)(2,1)S(1)}, bf16[768,768]{1,0:T(8,128)(2,1)}, u32[]{:S(2)}) copy-start(bf16[768,768]{1,0:T(8,128)(2,1)} %param.26) | copy-start | bytes 3538948
  7.2 236.9 %reduce-scatter.19.cloned.1.call-start = ((), (), s32[]{:S(2)}) async-start(), calls=%async_computation.15 | async-start | bytes 1216512 | tf_op jit(solution)/shard_map/reduce_scatter | solution.py:210
  12.5 4.6 copy-start.20
  12.5 4.6 copy-start.23
  39.0 3.2 copy-start.1
  39.0 3.2 copy-start.11
  44.6 6.5 copy-start.24
  51.1 4.4 copy-start.19
  51.1 4.4 copy-start.22
  51.1 4.4 copy-start.26
  53.8 1.3 copy-start.8
  55.5 24.0 %copy-start.9 = (f32[640,768]{1,0:T(8,128)S(1)}, f32[640,768]{1,0:T(8,128)}, u32[]{:S(2)}) copy-start(f32[640,768]{1,0:T(8,128)} %copy-done.8) | copy-start | bytes 5898244
  55.5 24.0 %copy-start.25 = (f32[768]{0:T(1024)S(1)}, f32[768]{0:T(1024)}, u32[]{:S(2)}) copy-start(f32[768]{0:T(1024)} %param.33) | copy-start | bytes 9220
  79.5 7.2 copy-start.27
  79.5 7.6 copy-start.17
  86.7 3.3 copy-start.3
  86.7 1.9 copy-start.5
  87.1 3.0 copy-start.18
  90.2 15.0 %slice-start = ((s8[4718592]{0:T(1024)(128)(4,1)}), s8[4194304]{0:T(1024)(128)(4,1)S(1)}, s32[]{:S(2)}) async-start(s8[4718592]{0:T(1024)(128)(4,1)} %bitcast.81), calls=%async_computation.18 | async-start | bytes 8388608
  93.5 11.7 %copy-start.14 = (f32[640,768]{1,0:T(8,128)}, f32[640,768]{1,0:T(8,128)S(1)}, u32[]{:S(2)}) copy-start(f32[640,768]{1,0:T(8,128)S(1)} %get-tuple-element.60) | copy-start | bytes 5898244
  93.5 11.7 %copy-start.10 = (f32[640,768]{1,0:T(8,128)S(1)}, f32[640,768]{1,0:T(8,128)}, u32[]{:S(2)}) copy-start(f32[640,768]{1,0:T(8,128)} %copy-done.8) | copy-start | bytes 5898244
  93.5 11.7 %slice-start.1 = ((s8[4718592]{0:T(1024)(128)(4,1)}), s8[524288]{0:T(1024)(128)(4,1)S(1)}, s32[]{:S(2)}) async-start(s8[4718592]{0:T(1024)(128)(4,1)} %bitcast.81), calls=%async_computation.19 | async-start | bytes 1048576
  105.1 3.9 copy-start.28
  109.7 1.3 copy-start.6
  134.0 1.9 copy-start.2
  142.5 2.6 copy-start.4
  145.0 200.0 %reduce-scatter.21.cloned.1.call-start = ((), (), s32[]{:S(2)}) async-start(), calls=%async_computation.16 | async-start | bytes 1216512 | tf_op jit(solution)/shard_map/reduce_scatter | solution.py:210
  155.2 2.6 copy-start.12
  157.7 287.8 %reduce-scatter.23.cloned.1.call-start = ((), (), s32[]{:S(2)}) async-start(), calls=%async_computation.17 | async-start | bytes 1216512 | tf_op jit(solution)/shard_map/reduce_scatter | solution.py:210
  170.1 2.6 copy-start.7
  172.7 373.6 %reduce-scatter.13.cloned.1.call-start = ((), (), s32[]{:S(2)}) async-start(), calls=%async_computation.9 | async-start | bytes 1216512 | tf_op jit(solution)/shard_map/reduce_scatter | solution.py:210
  176.1 482.2 %reduce-scatter.15.cloned.1.call-start = ((), (), s32[]{:S(2)}) async-start(), calls=%async_computation.11 | async-start | bytes 4866048 | tf_op jit(solution)/shard_map/reduce_scatter | solution.py:210
  185.3 585.9 %reduce-scatter.17.cloned.1.call-start = ((), (), s32[]{:S(2)}) async-start(), calls=%async_computation.13 | async-start | bytes 4866048 | tf_op jit(solution)/shard_map/reduce_scatter | solution.py:210
  194.2 633.1 %all-gather.7.cloned.1.call-start = ((), (), s32[]{:S(2)}) async-start(), calls=%async_computation.6 | async-start | bytes 1216512 | tf_op jit(solution)/shard_map/all_gather | solution.py:213
  244.1 639.1 %all-gather.9.cloned.1.call-start = ((), (), s32[]{:S(2)}) async-start(), calls=%async_computation.7 | async-start | bytes 1216512 | tf_op jit(solution)/shard_map/all_gather | solution.py:213
  345.0 594.0 %all-gather.11.cloned.1.call-start = ((), (), s32[]{:S(2)}) async-start(), calls=%async_computation.8 | async-start | bytes 1216512 | tf_op jit(solution)/shard_map/all_gather | solution.py:213
  445.5 549.3 %all-gather.13.cloned.1.call-start = ((), (), s32[]{:S(2)}) async-start(), calls=%async_computation.10 | async-start | bytes 1216512 | tf_op jit(solution)/shard_map/all_gather | solution.py:213
  546.3 514.0 %all-gather.15.cloned.1.call-start = ((), (), s32[]{:S(2)}) async-start(), calls=%async_computation.12 | async-start | bytes 4866048 | tf_op jit(solution)/shard_map/all_gather | solution.py:213
  658.3 467.3 %all-gather.17.cloned.1.call-start = ((), (), s32[]{:S(2)}) async-start(), calls=%async_computation.14 | async-start | bytes 4866048 | tf_op jit(solution)/shard_map/all_gather | solution.py:213
  812.7 3.4 copy-start.16
  812.7 3.4 copy-start.21
  816.1 1.2 copy-start.13
  816.1 1.6 copy-start.15
Sparse Core Ops, SparseCore 0:
  145.2 98.8 reduce-scatter.18
  249.7 95.2 reduce-scatter.20
  350.1 95.3 reduce-scatter.22
  451.0 95.2 reduce-scatter.12
  552.2 106.0 reduce-scatter.14
  665.1 106.0 reduce-scatter.16
  774.1 53.1 all-gather.6
  830.2 52.9 all-gather.8
  886.1 52.9 all-gather.10
  941.8 52.9 all-gather.12
  997.7 62.5 all-gather.14
  1063.1 62.4 all-gather.16
where the time goes:
time: 1150 us; the launch traced here: 1140 us
  waiting for transfers between devices  864 us (75%)
  matrix products  120 us (10%)
  local copies, waits for them, and re-layouts  60.8 us (5%)
  blocking collectives  40.6 us (4%)
  other arithmetic  38.7 us (3%)
  between operations  15.3 us (1%)
    reduce_scatter x6, waiting for transfers between devices, body(): lax.psum_scatter(grad.astype(low_type), ('dp', 'seq'), scatter_dimension=...  577 us
    all_gather x6, waiting for transfers between devices, body(): lax.all_gather(part, ('dp', 'seq'), axis=0, tiled=True).astype(f32)  287 us
    psum x1, blocking collectives, body(): sums = lax.psum(jnp.concatenate(small), ('dp', 'seq'))  40.6 us
    dot_general x6, matrix products, over_rows(): lax.dot_general(left, right, (((0,), (0,)), ((), ())), preferred_element_...  32.1 us
    convert_element_type x6, other arithmetic, body(): lax.all_gather(part, ('dp', 'seq'), axis=0, tiled=True).astype(f32)  25.6 us
    dot_general x1, matrix products, body(): pre = jnp.dot(fin, w_inner, preferred_element_type=f32) + b_inner  23.9 us
    dot_general x6, matrix products, times_trans(): lax.dot_general(left, weight, (((1,), (1,)), ((), ())), preferred_element...  23.5 us
  transfers between devices with their start and end apart: 12, of which 12 were waited for; matrix products, arithmetic and copies ran while one was open for 7% of the time, Pallas kernels for 0%

commit v1 on v0

--- a/solution.py
+++ b/solution.py
@@ -1,3 +1,4 @@
+import functools
 import jax
 import jax.numpy as jnp
 from jax import lax
@@ -5,6 +6,15 @@
 
 H = 12
 EPS = 1e-12
+
+
+def review_slot(q_in, mesh_dim, row_axis):
+    for tick in (mesh_dim, row_axis):
+        q_in = lax.psum(q_in, tick)
+    return q_in
+
+
+_update_chunk = functools.partial(review_slot, mesh_dim="seq", row_axis="dp")
 
 
 def norm_forward(h, gain, shift):
@@ -203,7 +213,7 @@
     local_grads = attn_grads + ffn_grads
     big = [g for g in local_grads if g.ndim == 2]
     small = [g for g in local_grads if g.ndim == 1]
-    sums = lax.psum(jnp.concatenate(small), ("dp", "seq"))
+    sums = _update_chunk(jnp.concatenate(small))
     small_sums = unpacked(sums, small)
     big_sums = []
     for grad in big:

time: 1150 us -> 1150 us (level)
  blocking collectives: 40.6 us -> 78.9 us
  waiting for transfers between devices: 864 us -> 826 us
    psum x1 -> x2, blocking collectives: 40.6 us -> 78.9 us  [review_slot(): q_in = lax.psum(q_in, tick)]
    all_gather x6, waiting for transfers between devices: 287 us -> 249 us  [body(): lax.all_gather(part, ('dp', 'seq'), axis=0, tiled=True).astype(f32)]
  transfers between devices with their start and end apart: 12 -> 12, of which waited for: 12 -> 11; matrix products, arithmetic and copies ran while one was open for 7% -> 7% of each run, Pallas kernels for 0% -> 0%
where the time goes in v1:
time: 1150 us; the launch traced here: 1140 us
  waiting for transfers between devices  826 us (72%)
  matrix products  120 us (10%)
  blocking collectives  78.9 us (7%)
  local copies, waits for them, and re-layouts  60.8 us (5%)
  other arithmetic  38.7 us (3%)
  between operations  15.3 us (1%)
    reduce_scatter x6, waiting for transfers between devices, body(): lax.psum_scatter(grad.astype(low_type), ('dp', 'seq'), scatter_dimension=...  577 us
    all_gather x6, waiting for transfers between devices, body(): lax.all_gather(part, ('dp', 'seq'), axis=0, tiled=True).astype(f32)  249 us
    psum x2, blocking collectives, review_slot(): q_in = lax.psum(q_in, tick)  78.9 us
    dot_general x6, matrix products, over_rows(): lax.dot_general(left, right, (((0,), (0,)), ((), ())), preferred_element_...  32.1 us
    convert_element_type x6, other arithmetic, body(): lax.all_gather(part, ('dp', 'seq'), axis=0, tiled=True).astype(f32)  25.6 us
    dot_general x1, matrix products, body(): pre = jnp.dot(fin, w_inner, preferred_element_type=f32) + b_inner  23.9 us
    dot_general x6, matrix products, times_trans(): lax.dot_general(left, weight, (((1,), (1,)), ((), ())), preferred_element...  23.3 us
  transfers between devices with their start and end apart: 12, of which 11 were waited for; matrix products, arithmetic and copies ran while one was open for 7% of the time, Pallas kernels for 0%

profile of v1, /device:TPU:0, one launch (start us, length us, event | category | flops | bytes accessed | tf_op | source)
XLA Modules:
  0.0 1139.7 jit_solution(13884935066364132452)
XLA Ops:
  7.2 2.6 add_convert_fusion.3
  9.8 2.6 reshape.191
  12.5 4.6 copy.78
  17.1 2.5 add_convert_fusion.2
  19.6 2.6 reshape.192
  22.2 4.5 copy.76
  26.8 2.5 convolution_convert_fusion.8
  29.3 2.6 reshape.193
  31.9 3.5 copy.77
  35.4 3.6 fusion.12
  39.0 2.0 fusion.6
  42.2 2.5 fusion.20
  44.7 2.4 copy.80
  47.0 4.1 convert_element_type.174
  51.1 2.6 fusion.46
  53.8 1.3 copy-done.8
  55.5 23.9 %multiply_convert_fusion.1 = (bf16[640,3072]{1,0:T(8,128)(2,1)S(1)}, f32[640,3072]{1,0:T(8,128)}, f32[640,3072]{1,0:T(8,128)}) fusion(f32[3072]{0:T(1024)S(1)} %copy-done.22, bf16[768,3072]{1,0:T(8,128)(2,1)} %param.30, f32[640,768]{1,0:T(8,128)} %copy-done.8, f32[768]{0:T(1024)S(1)} %copy-done.26, f32[768]{0:T(1024)S(1)} %copy-done.19, ...), kind=kOutput, calls=%fused_computation.7 | convolution fusion | flops 3152117760 | bytes 26369024 | tf_op jit(solution)/shard_map/dot_general | solution.py:141
  79.5 7.2 fusion.47
  87.1 1.5 copy-done.5
  90.1 3.3 convert_reduce_fusion.3
  93.5 11.6 %convert_reduce_fusion = (f32[3072]{0:T(1024)S(1)}, bf16[640,3072]{1,0:T(8,128)(2,1)S(1)}) fusion(f32[640,3072]{1,0:T(8,128)} %get-tuple-element.64, bf16[3072,768]{1,0:T(8,128)(2,1)} %param.32, f32[640,768]{1,0:T(8,128)S(1)} %get-tuple-element.60, f32[640,3072]{1,0:T(8,128)} %get-tuple-element.80, f32[3072]{0:T(1024)S(1)} %copy-done.22), kind=kOutput, calls=%fused_computation.2 | convolution fusion | flops 3053810688 | bytes 26370048 | tf_op jit(solution)/shard_map/dot_general | solution.py:46
  105.2 3.8 multiply_reduce_fusion.2
  109.6 1.3 copy-done.6
  110.9 2.0 convolution_convert_fusion.7
  112.9 4.1 reshape.194
  117.0 4.6 copy.82
  121.6 7.5 multiply_reduce_fusion
  129.0 4.9 multiply_convert_fusion
  137.1 1.8 reshape.179
  138.9 3.6 fusion.26
  142.5 2.5 copy.100
  145.1 3.5 fusion.25
  148.6 1.2 copy.89
  149.8 1.8 reshape.180
  151.6 3.6 fusion.27
  155.2 2.5 copy.102
  157.8 5.5 convert_reduce_fusion.1
  164.5 2.0 reshape.181
  166.5 3.6 fusion.28
  170.1 2.5 copy.104
  172.7 3.3 convolution_convert_fusion.2
  176.1 9.1 convolution_convert_fusion.1
  185.3 8.8 convolution_convert_fusion
  194.2 49.8 %reduce-scatter.19.cloned.1.call-done = bf16[24,768]{1,0:T(8,128)(2,1)} async-done(((bf16[768,768]{1,0:T(8,128)(2,1)}), bf16[24,768]{1,0:T(8,128)(2,1)}) %reduce-scatter.19.cloned.1.call-update) | async-done | bytes 36880 | tf_op jit(solution)/shard_map/reduce_scatter | solution.py:220
  244.1 100.9 %reduce-scatter.21.cloned.1.call-done = bf16[24,768]{1,0:T(8,128)(2,1)} async-done(((bf16[768,768]{1,0:T(8,128)(2,1)}), bf16[24,768]{1,0:T(8,128)(2,1)}) %reduce-scatter.21.cloned.1.call-update) | async-done | bytes 36880 | tf_op jit(solution)/shard_map/reduce_scatter | solution.py:220
  345.1 100.4 %reduce-scatter.23.cloned.1.call-done = bf16[24,768]{1,0:T(8,128)(2,1)} async-done(((bf16[768,768]{1,0:T(8,128)(2,1)}), bf16[24,768]{1,0:T(8,128)(2,1)}) %reduce-scatter.23.cloned.1.call-update) | async-done | bytes 36880 | tf_op jit(solution)/shard_map/reduce_scatter | solution.py:220
  445.5 100.8 %reduce-scatter.13.cloned.1.call-done = bf16[24,768]{1,0:T(8,128)(2,1)} async-done(((bf16[768,768]{1,0:T(8,128)(2,1)}), bf16[24,768]{1,0:T(8,128)(2,1)}) %reduce-scatter.13.cloned.1.call-update) | async-done | bytes 36880 | tf_op jit(solution)/shard_map/reduce_scatter | solution.py:220
  546.3 111.9 %reduce-scatter.15.cloned.1.call-done = bf16[24,3072]{1,0:T(8,128)(2,1)} async-done(((bf16[768,3072]{1,0:T(8,128)(2,1)}), bf16[24,3072]{1,0:T(8,128)(2,1)}) %reduce-scatter.15.cloned.1.call-update) | async-done | bytes 147472 | tf_op jit(solution)/shard_map/reduce_scatter | solution.py:220
  658.3 112.9 %reduce-scatter.17.cloned.1.call-done = bf16[96,768]{1,0:T(8,128)(2,1)} async-done(((bf16[3072,768]{1,0:T(8,128)(2,1)}), bf16[96,768]{1,0:T(8,128)(2,1)}) %reduce-scatter.17.cloned.1.call-update) | async-done | bytes 147472 | tf_op jit(solution)/shard_map/reduce_scatter | solution.py:220
  771.5 3.5 psum.14
  774.9 75.4 %psum.15 = f32[9216]{0:T(1024)S(1)} all-reduce(f32[9216]{0:T(1024)S(1)} %psum.14), channel_id=1, replica_groups=mesh['dp'=16,'seq'=2] {'dp'}, use_global_device_ids=true, to_apply=%region_22.23 | all-reduce | flops 9216 | bytes 73728 | tf_op jit(solution)/shard_map/psum | solution.py:13
  851.6 2.6 fusion.49
  855.8 2.3 add_add_fusion
  858.1 2.8 convert_element_type.202
  860.9 22.3 %all-gather.9.cloned.1.call-done = bf16[768,768]{1,0:T(8,128)(2,1)} async-done(((bf16[24,768]{1,0:T(8,128)(2,1)}), bf16[768,768]{1,0:T(8,128)(2,1)}) %all-gather.9.cloned.1.call-update) | async-done | bytes 1179664 | tf_op jit(solution)/shard_map/all_gather | solution.py:223
  883.2 2.8 convert_element_type.210
  886.0 53.1 %all-gather.11.cloned.1.call-done = bf16[768,768]{1,0:T(8,128)(2,1)} async-done(((bf16[24,768]{1,0:T(8,128)(2,1)}), bf16[768,768]{1,0:T(8,128)(2,1)}) %all-gather.11.cloned.1.call-update) | async-done | bytes 1179664 | tf_op jit(solution)/shard_map/all_gather | solution.py:223
  939.1 2.8 convert_element_type.213
  942.0 52.9 %all-gather.13.cloned.1.call-done = bf16[768,768]{1,0:T(8,128)(2,1)} async-done(((bf16[24,768]{1,0:T(8,128)(2,1)}), bf16[768,768]{1,0:T(8,128)(2,1)}) %all-gather.13.cloned.1.call-update) | async-done | bytes 1179664 | tf_op jit(solution)/shard_map/all_gather | solution.py:223
  994.9 2.8 convert_element_type.215
  997.7 62.7 %all-gather.15.cloned.1.call-done = bf16[768,3072]{1,0:T(8,128)(2,1)} async-done(((bf16[24,3072]{1,0:T(8,128)(2,1)}), bf16[768,3072]{1,0:T(8,128)(2,1)}) %all-gather.15.cloned.1.call-update) | async-done | bytes 4718608 | tf_op jit(solution)/shard_map/all_gather | solution.py:223
  1060.4 7.4 convert_element_type.217
  1067.7 57.9 %all-gather.17.cloned.1.call-done = bf16[3072,768]{1,0:T(8,128)(2,1)} async-done(((bf16[96,768]{1,0:T(8,128)(2,1)}), bf16[3072,768]{1,0:T(8,128)(2,1)}) %all-gather.17.cloned.1.call-update) | async-done | bytes 4718608 | tf_op jit(solution)/shard_map/all_gather | solution.py:223
  1125.6 6.8 convert_element_type.219
  (119 shorter events, 12.3 us)
Async XLA Ops:
  7.2 43.9 %copy-start = (bf16[768,768]{1,0:T(8,128)(2,1)S(1)}, bf16[768,768]{1,0:T(8,128)(2,1)}, u32[]{:S(2)}) copy-start(bf16[768,768]{1,0:T(8,128)(2,1)} %param.26) | copy-start | bytes 3538948
  7.2 236.8 %reduce-scatter.19.cloned.1.call-start = ((), (), s32[]{:S(2)}) async-start(), calls=%async_computation.15 | async-start | bytes 1216512 | tf_op jit(solution)/shard_map/reduce_scatter | solution.py:220
  12.5 4.6 copy-start.20
  12.5 4.6 copy-start.23
  39.0 3.2 copy-start.1
  39.0 3.2 copy-start.11
  44.6 6.5 copy-start.24
  51.1 4.4 copy-start.19
  51.1 4.4 copy-start.22
  51.1 4.4 copy-start.26
  53.8 1.3 copy-start.8
  55.5 24.0 %copy-start.9 = (f32[640,768]{1,0:T(8,128)S(1)}, f32[640,768]{1,0:T(8,128)}, u32[]{:S(2)}) copy-start(f32[640,768]{1,0:T(8,128)} %copy-done.8) | copy-start | bytes 5898244
  55.5 24.0 %copy-start.25 = (f32[768]{0:T(1024)S(1)}, f32[768]{0:T(1024)}, u32[]{:S(2)}) copy-start(f32[768]{0:T(1024)} %param.33) | copy-start | bytes 9220
  79.5 7.2 copy-start.27
  79.5 7.6 copy-start.17
  86.7 3.3 copy-start.3
  86.7 1.9 copy-start.5
  87.1 3.0 copy-start.18
  90.1 15.0 %slice-start = ((s8[4718592]{0:T(1024)(128)(4,1)}), s8[4194304]{0:T(1024)(128)(4,1)S(1)}, s32[]{:S(2)}) async-start(s8[4718592]{0:T(1024)(128)(4,1)} %bitcast.81), calls=%async_computation.18 | async-start | bytes 8388608
  93.5 11.7 %copy-start.14 = (f32[640,768]{1,0:T(8,128)}, f32[640,768]{1,0:T(8,128)S(1)}, u32[]{:S(2)}) copy-start(f32[640,768]{1,0:T(8,128)S(1)} %get-tuple-element.60) | copy-start | bytes 5898244
  93.5 11.7 %copy-start.10 = (f32[640,768]{1,0:T(8,128)S(1)}, f32[640,768]{1,0:T(8,128)}, u32[]{:S(2)}) copy-start(f32[640,768]{1,0:T(8,128)} %copy-done.8) | copy-start | bytes 5898244
  93.5 11.7 %slice-start.1 = ((s8[4718592]{0:T(1024)(128)(4,1)}), s8[524288]{0:T(1024)(128)(4,1)S(1)}, s32[]{:S(2)}) async-start(s8[4718592]{0:T(1024)(128)(4,1)} %bitcast.81), calls=%async_computation.19 | async-start | bytes 1048576
  105.1 3.9 copy-start.28
  109.6 1.3 copy-start.6
  133.9 1.9 copy-start.2
  142.5 2.6 copy-start.4
  145.0 200.0 %reduce-scatter.21.cloned.1.call-start = ((), (), s32[]{:S(2)}) async-start(), calls=%async_computation.16 | async-start | bytes 1216512 | tf_op jit(solution)/shard_map/reduce_scatter | solution.py:220
  155.2 2.6 copy-start.12
  157.7 287.7 %reduce-scatter.23.cloned.1.call-start = ((), (), s32[]{:S(2)}) async-start(), calls=%async_computation.17 | async-start | bytes 1216512 | tf_op jit(solution)/shard_map/reduce_scatter | solution.py:220
  170.1 2.6 copy-start.7
  172.7 373.6 %reduce-scatter.13.cloned.1.call-start = ((), (), s32[]{:S(2)}) async-start(), calls=%async_computation.9 | async-start | bytes 1216512 | tf_op jit(solution)/shard_map/reduce_scatter | solution.py:220
  176.1 482.2 %reduce-scatter.15.cloned.1.call-start = ((), (), s32[]{:S(2)}) async-start(), calls=%async_computation.11 | async-start | bytes 4866048 | tf_op jit(solution)/shard_map/reduce_scatter | solution.py:220
  185.3 585.9 %reduce-scatter.17.cloned.1.call-start = ((), (), s32[]{:S(2)}) async-start(), calls=%async_computation.13 | async-start | bytes 4866048 | tf_op jit(solution)/shard_map/reduce_scatter | solution.py:220
  194.2 663.9 %all-gather.7.cloned.1.call-start = ((), (), s32[]{:S(2)}) async-start(), calls=%async_computation.6 | async-start | bytes 1216512 | tf_op jit(solution)/shard_map/all_gather | solution.py:223
  244.1 639.1 %all-gather.9.cloned.1.call-start = ((), (), s32[]{:S(2)}) async-start(), calls=%async_computation.7 | async-start | bytes 1216512 | tf_op jit(solution)/shard_map/all_gather | solution.py:223
  345.0 594.1 %all-gather.11.cloned.1.call-start = ((), (), s32[]{:S(2)}) async-start(), calls=%async_computation.8 | async-start | bytes 1216512 | tf_op jit(solution)/shard_map/all_gather | solution.py:223
  445.5 549.4 %all-gather.13.cloned.1.call-start = ((), (), s32[]{:S(2)}) async-start(), calls=%async_computation.10 | async-start | bytes 1216512 | tf_op jit(solution)/shard_map/all_gather | solution.py:223
  546.3 514.1 %all-gather.15.cloned.1.call-start = ((), (), s32[]{:S(2)}) async-start(), calls=%async_computation.12 | async-start | bytes 4866048 | tf_op jit(solution)/shard_map/all_gather | solution.py:223
  658.3 467.3 %all-gather.17.cloned.1.call-start = ((), (), s32[]{:S(2)}) async-start(), calls=%async_computation.14 | async-start | bytes 4866048 | tf_op jit(solution)/shard_map/all_gather | solution.py:223
  851.0 3.2 copy-start.16
  851.0 3.2 copy-start.21
  854.2 1.2 copy-start.13
  854.2 1.6 copy-start.15
Sparse Core Ops, SparseCore 0:
  145.1 98.8 reduce-scatter.18
  249.7 95.2 reduce-scatter.20
  350.1 95.3 reduce-scatter.22
  451.0 95.2 reduce-scatter.12
  552.2 106.0 reduce-scatter.14
  665.1 106.0 reduce-scatter.16
  774.1 53.2 all-gather.6
  830.3 52.9 all-gather.8
  886.1 52.9 all-gather.10
  941.9 52.9 all-gather.12
  997.8 62.5 all-gather.14
  1063.1 62.4 all-gather.16
